TPU v7x, 32 devices: a 4x4x1 block of a 4x4x8 slice. The times are simulated.
32 devices in a mesh: sys: 1 (over z), zdom: 4 (over y), ydom: 8 (over x, core).
Axes of the slice: x: 4, y: 4, z: 1, core: 2. Of those that a mesh axis runs over, the one named last changes fastest.
The devices are a block of a 4x4x8 slice.
Arguments:
- charge: float32 [262144], P(('sys', 'ydom', 'zdom'))
- real_mask: int32 [262144], P(('sys', 'ydom', 'zdom'))
- grid_idx: int32 [262144, 3], P(('sys', 'ydom', 'zdom'))
- spline_w: float32 [262144, 3, 4], P(('sys', 'ydom', 'zdom'))
- influence: float32 [216, 216, 216], P(('sys', 'ydom'), 'zdom')
Outputs:
- output 1: float32 [216, 216, 216], P(('sys', 'ydom'), 'zdom')
- output 2: float32 [1], P('sys')
All inputs are finite; a program needn't handle non-finite values.
Results may differ from a plain program's by a relative error of at most 0.001.
Values are sent between devices in bfloat16 or wider.
A program may use at most 768 MiB of HBM per device.

v0:
```python
import functools
import math

import jax
import jax.numpy as jnp
import numpy as np
from jax import lax
from jax.experimental import pallas as pl
from jax.experimental.pallas import tpu as pltpu
from jax.sharding import PartitionSpec as P

MESH = pl.DeviceIdType.MESH
TAPS = 4
LANES = 128
NT_DIMS = (((1,), (1,)), ((), ()))


def round_up(value, unit):
    return -(-value // unit) * unit


def split_const(matrix):
    high = matrix.astype(jnp.bfloat16)
    low = (matrix - high.astype(np.float64)).astype(jnp.bfloat16)
    return high, low


def split_value(value):
    high = value.astype(jnp.bfloat16)
    low = (value - high.astype(jnp.float32)).astype(jnp.bfloat16)
    return high, low


def dot_f32(left, right):
    return jnp.dot(left, right, preferred_element_type=jnp.float32)


def dot_nt(left, right):
    return lax.dot_general(left, right, NT_DIMS, preferred_element_type=jnp.float32)


def spread_kernel(grid_n, rows_y, chunk, group, charge_ref, mask_ref, idx_ref, w_ref, out_ref,
                  a_hi, a_lo, b_hi, b_lo, y_ref, z_ref):
    slots = charge_ref.shape[1]
    rows_a = a_hi.shape[0]
    top_a = round_up(grid_n, 16)
    out_ref[...] = jnp.zeros_like(out_ref)
    if top_a < rows_a:
        a_hi[top_a:, :] = jnp.zeros((rows_a - top_a, chunk), jnp.bfloat16)
        a_lo[top_a:, :] = jnp.zeros((rows_a - top_a, chunk), jnp.bfloat16)

    def tap_block(first_row, rows, positions, weights):
        row_id = lax.broadcasted_iota(jnp.int32, (rows, chunk), 0) + first_row
        value = jnp.where(row_id == positions[0], weights[0], 0.0)
        for tap in range(1, TAPS):
            value = jnp.where(row_id == positions[tap], weights[tap], value)
        return value

    def one_chunk(step, carry):
        cols = pl.ds(pl.multiple_of(step * chunk, chunk), chunk)
        weight = charge_ref[:, cols] * mask_ref[:, cols].astype(jnp.float32)
        base = [idx_ref[d:d + 1, cols] for d in range(3)]
        taps = [[w_ref[d, s:s + 1, cols] for s in range(TAPS)] for d in range(3)]
        taps[0] = [tap * weight for tap in taps[0]]
        pos_x = [base[0] + s for s in range(TAPS)]
        pos_x = [jnp.where(pos >= grid_n, pos - grid_n, pos) for pos in pos_x]
        pos_y = [base[1] + s for s in range(TAPS)]
        pos_z = [base[2] + s for s in range(TAPS)]
        for row in range(0, top_a, 16):
            high, low = split_value(tap_block(row, 16, pos_x, taps[0]))
            a_hi[row:row + 16, :] = high
            a_lo[row:row + 16, :] = low
        for row in range(0, y_ref.shape[0], 8):
            y_ref[row:row + 8, :] = tap_block(row, 8, pos_y, taps[1])
        for row in range(0, 64, 8):
            z_ref[row:row + 8, :] = tap_block(row, 8, pos_z, taps[2])
        for first in range(0, rows_y, group):
            for y in range(first, first + group):
                line_y = y_ref[y:y + 1, :]
                for row in range(0, 64, 16):
                    high, low = split_value(line_y * z_ref[row:row + 16, :])
                    b_hi[y * 64 + row:y * 64 + row + 16, :] = high
                    b_lo[y * 64 + row:y * 64 + row + 16, :] = low
            block = slice(first * 64, (first + group) * 64)
            out_ref[block, :] += (dot_nt(b_hi[block, :], a_hi[...]) + dot_nt(b_lo[block, :], a_hi[...])
                                  + dot_nt(b_hi[block, :], a_lo[...]))
        return carry

    lax.fori_loop(0, slots // chunk, one_chunk, 0)


def modes_kernel(sizes, q_ref, bc_ref, fx_hi, fx_lo, fy_hi, fy_lo, wz_hi, wz_lo, flip_ref, ek_ref, energy_ref,
                 send_x, recv_x, send_y, recv_y, send_m, recv_m, send_r, recv_r, part, sums_y, part_z, sums_z,
                 sem_sx, sem_rx, sem_sy, sem_ry, sem_sm, sem_rm, sem_row, sem_ey, sem_ez):
    grid_n, y_devs, z_devs, len_x, len_z, planes, rows_k, chunks = sizes
    me_y = lax.axis_index('ydom')
    me_z = lax.axis_index('zdom')
    away_y = y_devs - 1 - me_y
    away_z = z_devs - 1 - me_z
    row_z = lax.rem(z_devs - me_z, z_devs)
    mirror = {'ydom': away_y, 'zdom': away_z}
    mirror_row = {'ydom': away_y, 'zdom': row_z}
    ring_y = [lax.rem(me_y + k, y_devs) for k in range(y_devs)]
    ring_z = [lax.rem(me_z + k, z_devs) for k in range(z_devs)]

    barrier = pltpu.get_barrier_semaphore()
    peers = [{'ydom': dest} for dest in ring_y[1:]] + [{'zdom': dest} for dest in ring_z[1:]] + [mirror, mirror_row]
    for peer in peers:
        pl.semaphore_signal(barrier, inc=1, device_id=peer, device_id_type=MESH)

    def remote(src, dst, send_sem, recv_sem, peer):
        return pltpu.make_async_remote_copy(src_ref=src, dst_ref=dst, send_sem=send_sem, recv_sem=recv_sem,
                                            device_id=peer, device_id_type=MESH)

    lane = lax.broadcasted_iota(jnp.int32, (1, LANES), 1)
    is_low = lane < 64
    all_kx = y_devs * planes

    for quad in range(q_ref.shape[0] // 256):
        high, low = split_value(q_ref[quad * 256:(quad + 1) * 256, :])
        block = dot_nt(fx_hi[...], high) + dot_nt(fx_lo[...], high) + dot_nt(fx_hi[...], low)
        for half in range(2):
            real = block[:all_kx, half * LANES:(half + 1) * LANES]
            imag = block[all_kx:, half * LANES:(half + 1) * LANES]
            y = 4 * quad + 2 * half
            send_x[pl.ds(y, all_kx, stride=32), :] = jnp.where(is_low, real, pltpu.roll(imag, 64, 1))
            send_x[pl.ds(y + 1, all_kx, stride=32), :] = jnp.where(is_low, pltpu.roll(real, 64, 1), imag)

    pl.semaphore_wait(barrier, len(peers))

    copies_x = []
    for c, (first, last) in enumerate(chunks):
        rows = (last - first) * 32
        group = []
        for k in range(1, y_devs):
            start = pl.multiple_of(ring_y[k] * (planes * 32) + first * 32, 32)
            copy = remote(send_x.at[pl.ds(start, rows), :], recv_x.at[me_y, pl.ds(first * 32, rows), :],
                          sem_sx.at[c, k], sem_rx.at[c, k], {'ydom': ring_y[k]})
            copy.start()
            group.append(copy)
        copies_x.append(group)
    recv_x[me_y] = send_x[pl.ds(pl.multiple_of(me_y * (planes * 32), 32), planes * 32), :]

    sign = jnp.where(is_low, 1.0, -1.0)
    half_ky = z_devs * rows_k
    copies_y = []
    for c, (first, last) in enumerate(chunks):
        for copy in copies_x[c]:
            copy.wait_recv()
        for p in range(first, last, 2):
            cols = []
            for kx in (p, p + 1):
                cols.append(jnp.concatenate([recv_x[s, kx * 32:(kx + 1) * 32, :] for s in range(y_devs)], axis=0))
            high, low = split_value(jnp.concatenate(cols, axis=1))
            block = dot_f32(fy_hi[...], high) + dot_f32(fy_lo[...], high) + dot_f32(fy_hi[...], low)
            for n, kx in enumerate((p, p + 1)):
                cos_part = block[:half_ky, n * LANES:(n + 1) * LANES]
                sin_part = block[half_ky:, n * LANES:(n + 1) * LANES]
                value = cos_part + pltpu.roll(sin_part, 64, 1) * sign
                for dest in range(z_devs):
                    send_y[dest, kx * rows_k:(kx + 1) * rows_k, :] = value[dest * rows_k:(dest + 1) * rows_k, :]
        rows = slice(first * rows_k, last * rows_k)
        group = []
        for k in range(1, z_devs):
            copy = remote(send_y.at[ring_z[k], rows, :], recv_y.at[me_z, rows, :],
                          sem_sy.at[c, k], sem_ry.at[c, k], {'zdom': ring_z[k]})
            copy.start()
            group.append(copy)
        copies_y.append(group)
        recv_y[me_z, rows, :] = send_y[me_z, rows, :]

    width = wz_hi.shape[1] // 4
    total = jnp.zeros((len_z, grid_n), jnp.float32)
    send_r[...] = jnp.zeros_like(send_r)
    copies_m = []
    for c, (first, last) in enumerate(chunks):
        for copy in copies_y[c]:
            copy.wait_recv()
        rows = slice(first * rows_k, last * rows_k)
        high, low = split_value(jnp.concatenate([recv_y[s, rows, :] for s in range(z_devs)], axis=1))
        block = dot_f32(high, wz_hi[...]) + dot_f32(low, wz_hi[...]) + dot_f32(high, wz_lo[...])
        parts = [block[:, n * width:(n + 1) * width] for n in range(4)]
        power = parts[0] * parts[0] + parts[1] * parts[1]
        power_rev = parts[2] * parts[2] + parts[3] * parts[3]
        for kx in range(first, last):
            at = (kx - first) * rows_k
            value = 0.5 * bc_ref[kx] * power[at:at + len_z, :grid_n]
            ek_ref[kx] = value
            total = total + value
            if kx >= 1:
                high, low = split_value(power_rev[at:at + rows_k, :])
                flipped = dot_f32(flip_ref[...], high) + dot_f32(flip_ref[...], low)
                send_m[kx] = flipped
                send_r[kx:kx + 1, :] = flipped[0:1, :]
        low_kx = max(first, 1)
        copy = remote(send_m.at[low_kx:last], recv_m.at[low_kx:last], sem_sm.at[c], sem_rm.at[c], mirror)
        copy.start()
        copies_m.append(copy)
    copy_row = remote(send_r, recv_r, sem_row.at[0], sem_row.at[1], mirror_row)
    copy_row.start()

    copy_row.wait_recv()
    is_first = lax.broadcasted_iota(jnp.int32, (len_z, grid_n), 0) == 0
    for c, (first, last) in enumerate(chunks):
        copies_m[c].wait_recv()
        for kx in range(max(first, 1), last):
            plane = len_x - kx
            power = jnp.where(is_first, recv_r[kx:kx + 1, :grid_n], recv_m[kx, :len_z, :grid_n])
            value = 0.5 * bc_ref[plane] * power
            ek_ref[plane] = value
            total = total + value

    def spread_sum(value, out, sums, send_sems, axis, ring, me):
        out[...] = jnp.zeros_like(out) + value
        copies = []
        for k in range(1, len(ring)):
            copy = remote(out, sums.at[me], send_sems.at[0, k], send_sems.at[1, k], {axis: ring[k]})
            copy.start()
            copies.append(copy)
        sums[me] = jnp.zeros(out.shape, jnp.float32) + value
        for copy in copies:
            copy.wait_recv()
        result = sums[0]
        for s in range(1, len(ring)):
            result = result + sums[s]
        return result, copies

    local = jnp.sum(total, keepdims=True)
    over_z, copies_ez = spread_sum(local, part, sums_z, sem_ez, 'zdom', ring_z, me_z)
    over_all, copies_ey = spread_sum(over_z, part_z, sums_y, sem_ey, 'ydom', ring_y, me_y)
    energy_ref[...] = over_all / (grid_n * grid_n * grid_n)

    for copy in [x for g in copies_x for x in g] + [x for g in copies_y for x in g] + copies_m + [copy_row]:
        copy.wait_send()
    for copy in copies_ez + copies_ey:
        copy.wait_send()


def transforms(grid_n, y_devs, z_devs, len_x, len_y, len_z, planes, rows_k):
    unit = 2.0 * math.pi / grid_n

    def angle(freq, pos):
        return ((freq[:, None] * pos[None, :]) % grid_n) * unit

    freq = (np.arange(y_devs)[:, None] * len_x + np.arange(planes)[None, :]).reshape(-1)
    phase = angle(freq, np.arange(grid_n))
    mat_x = np.zeros((2 * y_devs * planes, 256))
    mat_x[:, :grid_n] = np.concatenate([np.cos(phase), -np.sin(phase)])
    pos = (np.arange(y_devs)[:, None] * len_y + np.arange(32)[None, :]).reshape(-1)
    used = np.tile(np.arange(32) < len_y + TAPS - 1, y_devs)
    ky = (np.arange(z_devs)[:, None] * len_z + np.arange(rows_k)[None, :]).reshape(-1)
    keep = np.tile(np.arange(rows_k) < len_z, z_devs)
    phase = angle(ky, pos)
    mask = keep[:, None] * used[None, :]
    mat_y = np.concatenate([np.cos(phase) * mask, np.sin(phase) * mask])
    pos = np.arange(64)
    used = pos < len_z + TAPS - 1
    width = round_up(grid_n, LANES)
    mat_z = np.zeros((z_devs, 2, 64, 4, width))
    for dev in range(z_devs):
        phase = angle(dev * len_z + pos, np.arange(grid_n))
        cos_part = np.cos(phase) * used[:, None]
        sin_part = np.sin(phase) * used[:, None]
        mat_z[dev, 0, :, 0, :grid_n] = cos_part
        mat_z[dev, 1, :, 0, :grid_n] = sin_part
        mat_z[dev, 0, :, 1, :grid_n] = -sin_part
        mat_z[dev, 1, :, 1, :grid_n] = cos_part
        mat_z[dev, 0, :, 2, :grid_n] = cos_part
        mat_z[dev, 1, :, 2, :grid_n] = -sin_part
        mat_z[dev, 0, :, 3, :grid_n] = sin_part
        mat_z[dev, 1, :, 3, :grid_n] = cos_part
    mat_z = mat_z.reshape(z_devs * 128, 4 * width)
    flip = np.zeros((rows_k, rows_k))
    flip[0, 0] = 1.0
    flip[np.arange(1, len_z), len_z - np.arange(1, len_z)] = 1.0
    return (*split_const(mat_x), *split_const(mat_y), *split_const(mat_z), flip.astype(jnp.bfloat16))


def solution(mesh):
    y_devs = mesh.shape['ydom']
    z_devs = mesh.shape['zdom']
    slot_spec = P(('sys', 'ydom', 'zdom'))
    mode_spec = P(('sys', 'ydom'), 'zdom', None)

    def local_energy(charge, real_mask, grid_idx, spline_w, influence):
        len_x, len_k, grid_n = influence.shape
        len_y = grid_n // y_devs
        len_z = grid_n // z_devs
        slots = charge.shape[0]
        chunk = min(1024, slots)
        rows_y = len_y + TAPS - 1
        group = 10
        width = round_up(grid_n, LANES)
        vmem = pl.BlockSpec(memory_space=pltpu.VMEM)

        spread = pl.pallas_call(
            functools.partial(spread_kernel, grid_n, rows_y, chunk, group),
            name='spread',
            out_shape=jax.ShapeDtypeStruct((32 * 64, width), jnp.float32),
            in_specs=[vmem] * 4,
            out_specs=vmem,
            scratch_shapes=[
                pltpu.VMEM((width, chunk), jnp.bfloat16),
                pltpu.VMEM((width, chunk), jnp.bfloat16),
                pltpu.VMEM((rows_y * 64, chunk), jnp.bfloat16),
                pltpu.VMEM((rows_y * 64, chunk), jnp.bfloat16),
                pltpu.VMEM((32, chunk), jnp.float32),
                pltpu.VMEM((64, chunk), jnp.float32),
            ],
            compiler_params=pltpu.CompilerParams(vmem_limit_bytes=40 * 2**20),
        )
        grid_q = spread(charge.reshape(1, slots), real_mask.reshape(1, slots), grid_idx.T,
                        jnp.transpose(spline_w, (1, 2, 0)))

        planes = (len_x + 1) // 2
        rows_k = round_up(len_k, 8)
        chunks = tuple((p, min(p + 4, planes)) for p in range(0, planes, 4))
        sizes = (grid_n, y_devs, z_devs, len_x, len_z, planes, rows_k, chunks)
        mats = transforms(grid_n, y_devs, z_devs, len_x, len_y, len_z, planes, rows_k)
        f32 = jnp.float32
        n = len(chunks)
        dma = pltpu.SemaphoreType.DMA
        modes = pl.pallas_call(
            functools.partial(modes_kernel, sizes),
            name='modes',
            out_shape=(jax.ShapeDtypeStruct(influence.shape, f32), jax.ShapeDtypeStruct((8, LANES), f32)),
            in_specs=[vmem] * (2 + len(mats)),
            out_specs=(vmem, vmem),
            scratch_shapes=[
                pltpu.VMEM((y_devs * planes * 32, LANES), f32),
                pltpu.VMEM((y_devs, planes * 32, LANES), f32),
                pltpu.VMEM((z_devs, planes * rows_k, LANES), f32),
                pltpu.VMEM((z_devs, planes * rows_k, LANES), f32),
                pltpu.VMEM((planes, rows_k, width), f32),
                pltpu.VMEM((planes, rows_k, width), f32),
                pltpu.VMEM((round_up(planes, 8), width), f32),
                pltpu.VMEM((round_up(planes, 8), width), f32),
                pltpu.VMEM((8, LANES), f32),
                pltpu.VMEM((y_devs, 8, LANES), f32),
                pltpu.VMEM((8, LANES), f32),
                pltpu.VMEM((z_devs, 8, LANES), f32),
                dma((n, y_devs)), dma((n, y_devs)), dma((n, z_devs)), dma((n, z_devs)),
                dma((n,)), dma((n,)), dma((2,)), dma((2, y_devs)), dma((2, z_devs)),
            ],
            compiler_params=pltpu.CompilerParams(collective_id=0, has_side_effects=True,
                                                 vmem_limit_bytes=56 * 2**20),
        )
        mode_energy, energy = modes(grid_q, influence, *mats)
        return mode_energy, energy[0, :1]

    return jax.shard_map(local_energy, mesh=mesh, in_specs=(slot_spec, slot_spec, P(('sys', 'ydom', 'zdom'), None), P(('sys', 'ydom', 'zdom'), None, None), mode_spec), out_specs=(mode_spec, P('sys')), check_vma=False)
```

profile of v0, /device:TPU:97, one launch (start us, length us, event | category | flops | bytes accessed | tf_op | source)
XLA Modules:
  0.0 112.5 jit_solution(16748479506015483353)
XLA Ops:
  0.6 0.0 copy-start.1
  0.6 1.0 copy-done.1
  1.6 0.0 copy-start.2
  1.6 0.9 copy-done.2
  2.5 0.0 copy-start.3
  2.5 0.8 copy-done.3
  3.3 0.0 copy-start.4
  3.3 0.8 copy-done.4
  4.0 29.8 %spread.1.q_ref = f32[2048,256]{1,0:T(8,128)S(1)} custom-call(f32[1,8192]{1,0:T(1,128)S(1)} %bitcast.7, s32[1,8192]{1,0:T(1,128)S(1)} %bitcast.8, s32[3,8192]{1,0:T(4,128)S(1)} %bitcast.6, f32[3,4,8192]{2,1,0:T(4,128)S(1)} %bitcast.5), custom_call_target="tpu_custom_call" | custom-call | tf_op jit(solution)/shard_map/spread/pallas_call | solution.py:312
  33.8 0.0 copy-start
  33.9 1.3 %copy-done = f32[2048,256]{1,0:T(8,128)} copy-done((f32[2048,256]{1,0:T(8,128)}, f32[2048,256]{1,0:T(8,128)S(1)}, u32[]{:S(2)}) %copy-start) | copy-done | bytes 2097176
  35.2 73.4 %modes.1 = (f32[27,54,216]{2,1,0:T(8,128)}, f32[8,128]{1,0:T(8,128)}) custom-call(f32[2048,256]{1,0:T(8,128)} %copy-done, f32[27,54,216]{2,1,0:T(8,128)} %bc_ref.1, bf16[224,256]{1,0:T(8,128)(2,1)} %constant.14.clone.fx_hi, bf16[224,256]{1,0:T(8,128)(2,1)} %constant.15.clone.fx_lo, bf16[448,256]{1,0:T(8,128)(2,1)} %constant.16.clone.fy_hi, ...), custom_call_target="tpu_custom_call" | custom-call | tf_op jit(solution)/shard_map/modes/pallas_call | solution.py:348
  108.6 1.2 %slice.3 = f32[1,1]{1,0:T(1,128)} slice(f32[8,128]{1,0:T(8,128)} %get-tuple-element.5), slice={[0:1], [0:1]} | slice | bytes 8 | tf_op jit(solution)/shard_map/slice | solution.py:349
  109.8 2.6 %copy.15 = f32[27,54,216]{2,1,0:T(8,128)} copy(f32[27,54,216]{2,1,0:T(8,128)} %get-tuple-element.8) | data formatting | bytes 2519424
Async XLA Ops:
  0.6 1.0 copy-start.1
  1.6 0.9 copy-start.2
  2.5 0.8 copy-start.3
  3.3 0.8 copy-start.4
  33.8 1.3 %copy-start = (f32[2048,256]{1,0:T(8,128)}, f32[2048,256]{1,0:T(8,128)S(1)}, u32[]{:S(2)}) copy-start(f32[2048,256]{1,0:T(8,128)S(1)} %spread.1.q_ref) | copy-start | bytes 6291460
where the time goes:
time: 113 us; the launch traced here: 112 us
  Pallas kernels  103 us (91%)
  local copies, waits for them, and re-layouts  8.56 us (8%)
    pallas_call x1, Pallas kernels, local_energy(): mode_energy, energy = modes(grid_q, influence, *mats)  73.4 us
    pallas_call x1, Pallas kernels, local_energy(): spread(charge.reshape(1, slots), real_mask.reshape(1, slots), grid_idx.T,...  29.8 us
    unnamed x11, local copies, waits for them, and re-layouts  7.37 us

commit v1 on v0

v1 whole, which is shorter than its diff:
```python
import functools
import math

import jax
import jax.numpy as jnp
import numpy as np
from jax import lax
from jax.experimental import pallas as pl
from jax.experimental.pallas import tpu as pltpu
from jax.sharding import PartitionSpec as P

MESH = pl.DeviceIdType.MESH
TAPS = 4
LANES = 128
NT_DIMS = (((1,), (1,)), ((), ()))


def round_up(value, unit):
    return -(-value // unit) * unit


def split_const(matrix):
    high = matrix.astype(jnp.bfloat16)
    low = (matrix - high.astype(np.float64)).astype(jnp.bfloat16)
    return high, low


def split_value(value):
    high = value.astype(jnp.bfloat16)
    low = (value - high.astype(jnp.float32)).astype(jnp.bfloat16)
    return high, low


def dot_f32(left, right):
    return jnp.dot(left, right, preferred_element_type=jnp.float32)


def dot_nt(left, right):
    return lax.dot_general(left, right, NT_DIMS, preferred_element_type=jnp.float32)


def encode(value, code_lane):
    lane = lax.broadcasted_iota(jnp.int32, (1, value.shape[1]), 1)
    top = jnp.max(jnp.abs(value), axis=1, keepdims=True)
    code = jnp.ceil(jnp.log2(jnp.maximum(top, 1e-35)) * 64.0) + 1.0
    steps = jnp.round(value * (jnp.exp2(code * (-1.0 / 64.0)) * 32766.0))
    return jnp.where(lane == code_lane, code, steps).astype(jnp.int32).astype(jnp.int16)


def decode(packed, code_lane):
    lane = lax.broadcasted_iota(jnp.int32, (1, packed.shape[1]), 1)
    steps = packed.astype(jnp.int32).astype(jnp.float32)
    code = steps[:, code_lane:code_lane + 1]
    return jnp.where(lane == code_lane, 0.0, steps * (jnp.exp2(code * (1.0 / 64.0)) * (1.0 / 32766.0)))


CODE = 63


def energy_kernel(sizes, charge_ref, mask_ref, idx_ref, w_ref, bc_hbm, fx_hi, fx_lo, fy_hi, fy_lo, wz_hi, wz_lo, flip_hbm,
                  ek_ref, energy_ref,
                  a_hi, a_lo, b_hi0, b_lo0, b_hi1, b_lo1, y_ref, z_ref, q_ref, wide_x,
                  bc_ref, fxh, fxl, fyh, fyl, wzh, wzl, flip_ref,
                  send_x, recv_x, send_y, recv_y, send_m, recv_m, send_r, recv_r, part, sums_y, part_z, sums_z,
                  sem_in, sem_sx, sem_rx, sem_sy, sem_ry, sem_sm, sem_rm, sem_row, sem_ey, sem_ez):
    grid_n, y_devs, z_devs, len_x, len_z, planes, rows_k, chunks, groups, chunk = sizes
    me_y = lax.axis_index('ydom')
    me_z = lax.axis_index('zdom')
    away_y = y_devs - 1 - me_y
    away_z = z_devs - 1 - me_z
    row_z = lax.rem(z_devs - me_z, z_devs)
    mirror = {'ydom': away_y, 'zdom': away_z}
    mirror_row = {'ydom': away_y, 'zdom': row_z}
    ring_y = [lax.rem(me_y + k, y_devs) for k in range(y_devs)]
    ring_z = [lax.rem(me_z + k, z_devs) for k in range(z_devs)]

    barrier = pltpu.get_barrier_semaphore()
    peers = [{'ydom': dest} for dest in ring_y[1:]] + [{'zdom': dest} for dest in ring_z[1:]] + [mirror, mirror_row]
    for peer in peers:
        pl.semaphore_signal(barrier, inc=1, device_id=peer, device_id_type=MESH)

    loads = [pltpu.make_async_copy(src, dst, sem_in.at[n]) for n, (src, dst) in enumerate(
        [(fx_hi, fxh), (fx_lo, fxl), (fy_hi, fyh), (fy_lo, fyl), (wz_hi, wzh), (wz_lo, wzl), (flip_hbm, flip_ref),
         (bc_hbm, bc_ref)])]
    for load in loads:
        load.start()

    def remote(src, dst, send_sem, recv_sem, peer):
        return pltpu.make_async_remote_copy(src_ref=src, dst_ref=dst, send_sem=send_sem, recv_sem=recv_sem,
                                            device_id=peer, device_id_type=MESH)

    lane = lax.broadcasted_iota(jnp.int32, (1, LANES), 1)
    is_low = lane < 64
    all_kx = y_devs * planes
    per_dest = planes * 8

    slots = charge_ref.shape[1]
    n_chunks = slots // chunk
    rows_a = a_hi.shape[1]
    top_a = round_up(grid_n, 16)
    for c in range(n_chunks):
        for ref in (a_hi, a_lo):
            ref[c, top_a:, :] = jnp.zeros((rows_a - top_a, chunk), jnp.bfloat16)
    rows_y = y_ref.shape[1]

    def tap_block(first_row, rows, positions, weights):
        row_id = lax.broadcasted_iota(jnp.int32, (rows, chunk), 0) + first_row
        value = jnp.where(row_id == positions[0], weights[0], 0.0)
        for tap in range(1, TAPS):
            value = jnp.where(row_id == positions[tap], weights[tap], value)
        return value

    def make_lines(c):
        cols = pl.ds(pl.multiple_of(c * chunk, chunk), chunk)
        weight = charge_ref[:, cols] * mask_ref[:, cols].astype(jnp.float32)
        base = [idx_ref[d:d + 1, cols] for d in range(3)]
        taps = [[w_ref[d, s:s + 1, cols] for s in range(TAPS)] for d in range(3)]
        taps[0] = [tap * weight for tap in taps[0]]
        pos_x = [base[0] + s for s in range(TAPS)]
        pos_x = [jnp.where(pos >= grid_n, pos - grid_n, pos) for pos in pos_x]
        pos_y = [base[1] + s for s in range(TAPS)]
        pos_z = [base[2] + s for s in range(TAPS)]
        for row in range(0, rows_y, 8):
            y_ref[c, row:row + 8, :] = tap_block(row, 8, pos_y, taps[1])
        for row in range(0, 64, 8):
            z_ref[c, row:row + 8, :] = tap_block(row, 8, pos_z, taps[2])
        for row in range(0, top_a, 16):
            high, low = split_value(tap_block(row, 16, pos_x, taps[0]))
            a_hi[c, row:row + 16, :] = high
            a_lo[c, row:row + 16, :] = low

    def make_b(g, c, high_ref, low_ref):
        for y in range(8):
            line_y = y_ref[c, pl.ds(g * 8 + y, 1), :]
            for row in range(0, 64, 16):
                high, low = split_value(line_y * z_ref[c, row:row + 16, :])
                high_ref[y * 64 + row:y * 64 + row + 16, :] = high
                low_ref[y * 64 + row:y * 64 + row + 16, :] = low

    make_lines(0)
    make_b(0, 0, b_hi0, b_lo0)
    copies_x = []
    for g, in_group in enumerate(groups):
        used = slice(0, in_group * 64)
        q_ref[...] = jnp.zeros_like(q_ref)

        def add_chunk(c, high_ref, low_ref):
            high, low = a_hi[c], a_lo[c]
            q_ref[used, :] += (dot_nt(high_ref[used, :], high) + dot_nt(low_ref[used, :], high)
                               + dot_nt(high_ref[used, :], low))

        def pair(step, carry):
            after = 2 * step + 2
            wrap = after // n_chunks
            after_c = after - wrap * n_chunks
            if g == 0:
                make_lines(2 * step + 1)
            make_b(g, 2 * step + 1, b_hi1, b_lo1)
            add_chunk(2 * step, b_hi0, b_lo0)
            if g == 0:
                make_lines(after_c)
            make_b(g + wrap, after_c, b_hi0, b_lo0)
            add_chunk(2 * step + 1, b_hi1, b_lo1)
            return carry

        lax.fori_loop(0, n_chunks // 2, pair, 0)

        if g == 0:
            loads[0].wait()
            loads[1].wait()
        for quad in range(2):
            high, low = split_value(q_ref[quad * 256:(quad + 1) * 256, :])
            block = dot_nt(fxh[...], high) + dot_nt(fxl[...], high) + dot_nt(fxh[...], low)
            for half in range(2):
                real = block[:all_kx, half * LANES:(half + 1) * LANES]
                imag = block[all_kx:, half * LANES:(half + 1) * LANES]
                y = 4 * quad + 2 * half
                wide_x[pl.ds(y, all_kx, stride=8), :] = jnp.where(is_low, real, pltpu.roll(imag, 64, 1))
                wide_x[pl.ds(y + 1, all_kx, stride=8), :] = jnp.where(is_low, pltpu.roll(real, 64, 1), imag)

        def pack_rows(step, carry, g=g):
            rows = pl.ds(pl.multiple_of(step * per_dest, 16), per_dest)
            send_x[g, rows, :] = encode(wide_x[rows, :], CODE)
            return carry

        lax.fori_loop(0, y_devs, pack_rows, 0)
        if g == 0:
            pl.semaphore_wait(barrier, len(peers))
        for k in range(1, y_devs):
            start = pl.multiple_of(ring_y[k] * per_dest, 16)
            copy = remote(send_x.at[g, pl.ds(start, per_dest), :], recv_x.at[g, me_y],
                          sem_sx.at[g, k], sem_rx.at[g, k], {'ydom': ring_y[k]})
            copy.start()
            copies_x.append(copy)
        recv_x[g, me_y] = send_x[g, pl.ds(pl.multiple_of(me_y * per_dest, 16), per_dest), :]

    for load in loads[2:]:
        load.wait()
    for copy in copies_x:
        copy.wait_recv()

    sign = jnp.where(is_low, 1.0, -1.0)
    half_ky = z_devs * rows_k
    copies_y = []
    for c, (first, last) in enumerate(chunks):
        for p in range(first, last, 2):
            cols = [[], []]
            for g in range(len(groups)):
                for s in range(y_devs):
                    both = decode(recv_x[g, s, p * 8:(p + 2) * 8, :], CODE)
                    cols[0].append(both[:8])
                    cols[1].append(both[8:])
            wide = jnp.concatenate([jnp.concatenate(col, axis=0) for col in cols], axis=1)
            high, low = split_value(wide)
            block = dot_f32(fyh[...], high) + dot_f32(fyl[...], high) + dot_f32(fyh[...], low)
            values = []
            for n in range(2):
                cos_part = block[:half_ky, n * LANES:(n + 1) * LANES]
                sin_part = block[half_ky:, n * LANES:(n + 1) * LANES]
                values.append(cos_part + pltpu.roll(sin_part, 64, 1) * sign)
            for dest in range(z_devs):
                rows = slice(dest * rows_k, (dest + 1) * rows_k)
                both = jnp.concatenate([values[0][rows], values[1][rows]], axis=0)
                send_y[dest, p * rows_k:(p + 2) * rows_k, :] = encode(both, CODE)
        rows = slice(first * rows_k, last * rows_k)
        group = []
        for k in range(1, z_devs):
            copy = remote(send_y.at[ring_z[k], rows, :], recv_y.at[me_z, rows, :],
                          sem_sy.at[c, k], sem_ry.at[c, k], {'zdom': ring_z[k]})
            copy.start()
            group.append(copy)
        copies_y.append(group)
        recv_y[me_z, rows, :] = send_y[me_z, rows, :]

    width = wzh.shape[1] // 2
    total = jnp.zeros((len_z, grid_n), jnp.float32)
    send_r[...] = jnp.zeros_like(send_r)
    copies_m = []
    for c, (first, last) in enumerate(chunks):
        for copy in copies_y[c]:
            copy.wait_recv()
        rows = slice(first * rows_k, last * rows_k)
        high, low = split_value(jnp.concatenate([decode(recv_y[s, rows, :], CODE) for s in range(z_devs)], axis=1))
        is_real = jnp.concatenate([is_low] * z_devs, axis=1)
        nil = jnp.zeros_like(high)
        from_real, from_imag = [
            dot_f32(h, wzh[...]) + dot_f32(l, wzh[...]) + dot_f32(h, wzl[...])
            for h, l in ((jnp.where(is_real, high, nil), jnp.where(is_real, low, nil)),
                         (jnp.where(is_real, nil, high), jnp.where(is_real, nil, low)))]
        both_signs = [from_real + from_imag, from_real - from_imag]
        power, power_rev = [v[:, :width] * v[:, :width] + v[:, width:] * v[:, width:] for v in both_signs]
        for p in range(first, last, 2):
            both = []
            for kx in (p, p + 1):
                at = (kx - first) * rows_k
                value = 0.5 * bc_ref[kx] * power[at:at + len_z, :grid_n]
                ek_ref[kx] = value
                total = total + value
                high, low = split_value(power_rev[at:at + rows_k, :])
                flipped = dot_f32(flip_ref[...], high) + dot_f32(flip_ref[...], low)
                send_r[kx:kx + 1, :] = flipped[0:1, :]
                both.append(flipped)
            send_m[p * rows_k:(p + 2) * rows_k, :] = encode(jnp.concatenate(both, axis=0), width - 1)
        copy = remote(send_m.at[rows, :], recv_m.at[rows, :], sem_sm.at[c], sem_rm.at[c], mirror)
        copy.start()
        copies_m.append(copy)
    copy_row = remote(send_r, recv_r, sem_row.at[0], sem_row.at[1], mirror_row)
    copy_row.start()

    copy_row.wait_recv()
    is_first = lax.broadcasted_iota(jnp.int32, (len_z, grid_n), 0) == 0
    for c, (first, last) in enumerate(chunks):
        copies_m[c].wait_recv()
        for p in range(first, last, 2):
            both = decode(recv_m[p * rows_k:(p + 2) * rows_k, :], width - 1)
            for kx in (p, p + 1):
                if kx >= 1:
                    plane = len_x - kx
                    at = (kx - p) * rows_k
                    power = jnp.where(is_first, recv_r[kx:kx + 1, :grid_n], both[at:at + len_z, :grid_n])
                    value = 0.5 * bc_ref[plane] * power
                    ek_ref[plane] = value
                    total = total + value

    def spread_sum(value, out, sums, sems, axis, ring, me):
        out[...] = jnp.zeros_like(out) + value
        copies = []
        for k in range(1, len(ring)):
            copy = remote(out, sums.at[me], sems.at[0, k], sems.at[1, k], {axis: ring[k]})
            copy.start()
            copies.append(copy)
        sums[me] = jnp.zeros(out.shape, jnp.float32) + value
        for copy in copies:
            copy.wait_recv()
        result = sums[0]
        for s in range(1, len(ring)):
            result = result + sums[s]
        return result, copies

    local = jnp.sum(total, keepdims=True)
    over_z, copies_ez = spread_sum(local, part, sums_z, sem_ez, 'zdom', ring_z, me_z)
    over_all, copies_ey = spread_sum(over_z, part_z, sums_y, sem_ey, 'ydom', ring_y, me_y)
    energy_ref[0] = over_all[0, 0] / (grid_n * grid_n * grid_n)

    for copy in copies_x + [x for g in copies_y for x in g] + copies_m + [copy_row] + copies_ez + copies_ey:
        copy.wait_send()


def transforms(grid_n, y_devs, z_devs, len_x, len_y, len_z, planes, rows_k):
    unit = 2.0 * math.pi / grid_n

    def angle(freq, pos):
        return ((freq[:, None] * pos[None, :]) % grid_n) * unit

    freq = (np.arange(y_devs)[:, None] * len_x + np.arange(planes)[None, :]).reshape(-1)
    phase = angle(freq, np.arange(grid_n))
    mat_x = np.zeros((2 * y_devs * planes, 256))
    mat_x[:, :grid_n] = np.concatenate([np.cos(phase), -np.sin(phase)])
    local_y = np.broadcast_to(np.arange(32).reshape(4, 1, 8), (4, y_devs, 8)).reshape(-1)
    pos = np.broadcast_to(np.arange(y_devs).reshape(1, y_devs, 1) * len_y, (4, y_devs, 8)).reshape(-1) + local_y
    used = local_y < len_y + TAPS - 1
    ky = (np.arange(z_devs)[:, None] * len_z + np.arange(rows_k)[None, :]).reshape(-1)
    keep = np.tile(np.arange(rows_k) < len_z, z_devs)
    phase = angle(ky, pos)
    mask = keep[:, None] * used[None, :]
    mat_y = np.concatenate([np.cos(phase) * mask, np.sin(phase) * mask])
    pos = np.arange(64)
    used = pos < len_z + TAPS - 1
    width = round_up(grid_n, LANES)
    mat_z = np.zeros((z_devs, 2, 64, 2, width))
    for dev in range(z_devs):
        phase = angle(dev * len_z + pos, np.arange(grid_n))
        cos_part = np.cos(phase) * used[:, None]
        sin_part = np.sin(phase) * used[:, None]
        mat_z[dev, 0, :, 0, :grid_n] = cos_part
        mat_z[dev, 1, :, 0, :grid_n] = sin_part
        mat_z[dev, 0, :, 1, :grid_n] = -sin_part
        mat_z[dev, 1, :, 1, :grid_n] = cos_part
    mat_z = mat_z.reshape(z_devs * 128, 2 * width)
    flip = np.zeros((rows_k, rows_k))
    flip[0, 0] = 1.0
    flip[np.arange(1, len_z), len_z - np.arange(1, len_z)] = 1.0
    return (*split_const(mat_x), *split_const(mat_y), *split_const(mat_z), flip.astype(jnp.bfloat16))


def solution(mesh):
    y_devs = mesh.shape['ydom']
    z_devs = mesh.shape['zdom']
    slot_spec = P(('sys', 'ydom', 'zdom'))
    mode_spec = P(('sys', 'ydom'), 'zdom', None)

    def local_energy(charge, real_mask, grid_idx, spline_w, influence):
        len_x, len_k, grid_n = influence.shape
        len_y = grid_n // y_devs
        len_z = grid_n // z_devs
        slots = charge.shape[0]
        chunk = 1024
        rows_y = len_y + TAPS - 1
        groups = tuple(min(8, rows_y - y) for y in range(0, rows_y, 8))
        width = round_up(grid_n, LANES)
        planes = (len_x + 1) // 2
        rows_k = round_up(len_k, 8)
        chunks = tuple((p, min(p + 4, planes)) for p in range(0, planes, 4))
        sizes = (grid_n, y_devs, z_devs, len_x, len_z, planes, rows_k, chunks, groups, chunk)
        mats = transforms(grid_n, y_devs, z_devs, len_x, len_y, len_z, planes, rows_k)
        f32, bf16, i16 = jnp.float32, jnp.bfloat16, jnp.int16
        vmem = pl.BlockSpec(memory_space=pltpu.VMEM)
        anywhere = pl.BlockSpec(memory_space=pl.ANY)
        n, n_g, n_c = len(chunks), len(groups), slots // chunk
        dma = pltpu.SemaphoreType.DMA
        mode_energy, energy = pl.pallas_call(
            functools.partial(energy_kernel, sizes),
            name='energy',
            out_shape=(jax.ShapeDtypeStruct(influence.shape, f32), jax.ShapeDtypeStruct((1,), f32)),
            in_specs=[vmem] * 4 + [anywhere] * (1 + len(mats)),
            out_specs=(vmem, pl.BlockSpec(memory_space=pltpu.SMEM)),
            scratch_shapes=[
                pltpu.VMEM((n_c, width, chunk), bf16), pltpu.VMEM((n_c, width, chunk), bf16),
                pltpu.VMEM((512, chunk), bf16), pltpu.VMEM((512, chunk), bf16),
                pltpu.VMEM((512, chunk), bf16), pltpu.VMEM((512, chunk), bf16),
                pltpu.VMEM((n_c, 8 * n_g + 8, chunk), f32), pltpu.VMEM((n_c, 64, chunk), f32),
                pltpu.VMEM((512, width), f32), pltpu.VMEM((y_devs * planes * 8, LANES), f32),
                pltpu.VMEM(influence.shape, f32), *[pltpu.VMEM(mat.shape, mat.dtype) for mat in mats],
                pltpu.VMEM((n_g, y_devs * planes * 8, LANES), i16),
                pltpu.VMEM((n_g, y_devs, planes * 8, LANES), i16),
                pltpu.VMEM((z_devs, planes * rows_k, LANES), i16),
                pltpu.VMEM((z_devs, planes * rows_k, LANES), i16),
                pltpu.VMEM((planes * rows_k, width), i16),
                pltpu.VMEM((planes * rows_k, width), i16),
                pltpu.VMEM((round_up(planes, 8), width), f32),
                pltpu.VMEM((round_up(planes, 8), width), f32),
                pltpu.VMEM((8, LANES), f32),
                pltpu.VMEM((y_devs, 8, LANES), f32),
                pltpu.VMEM((8, LANES), f32),
                pltpu.VMEM((z_devs, 8, LANES), f32),
                dma((8,)), dma((n_g, y_devs)), dma((n_g, y_devs)), dma((n, z_devs)), dma((n, z_devs)),
                dma((n,)), dma((n,)), dma((2,)), dma((2, y_devs)), dma((2, z_devs)),
            ],
            compiler_params=pltpu.CompilerParams(collective_id=0, has_side_effects=True,
                                                 vmem_limit_bytes=60 * 2**20),
        )(charge.reshape(1, slots), real_mask.reshape(1, slots), grid_idx.T, jnp.transpose(spline_w, (1, 2, 0)),
          influence, *mats)
        return mode_energy, energy

    return jax.shard_map(local_energy, mesh=mesh, in_specs=(slot_spec, slot_spec, P(('sys', 'ydom', 'zdom'), None), P(('sys', 'ydom', 'zdom'), None, None), mode_spec), out_specs=(mode_spec, P('sys')), check_vma=False)
```

time: 113 us -> 96.8 us (0.86)
  Pallas kernels: 103 us -> 91.7 us
  local copies, waits for them, and re-layouts: 8.56 us -> 2.63 us
  between operations: 0.67 us -> 2.37 us
    pallas_call x2 -> x1, Pallas kernels: 103 us -> 91.7 us  [local_energy(): pl.pallas_call(functools.partial(energy_kernel, sizes), name='energy', ou...]
    unnamed x11 -> x1, local copies, waits for them, and re-layouts: 7.37 us -> 2.63 us
    slice x1 -> x0, local copies, waits for them, and re-layouts: 1.19 us -> none  [local_energy(): return (mode_energy, energy[0, :1])]
where the time goes in v1:
time: 96.8 us; the launch traced here: 96.7 us
  Pallas kernels  91.7 us (95%)
  local copies, waits for them, and re-layouts  2.63 us (3%)
  between operations  2.37 us (2%)
    pallas_call x1, Pallas kernels, local_energy(): pl.pallas_call(functools.partial(energy_kernel, sizes), name='energy', ou...  91.7 us
    unnamed x1, local copies, waits for them, and re-layouts  2.63 us

profile of v1, /device:TPU:97, one launch (start us, length us, event | category | flops | bytes accessed | tf_op | source)
XLA Modules:
  0.0 96.7 jit_solution(6373839481151624019)
XLA Ops:
  0.6 91.7 %energy.1 = (f32[27,54,216]{2,1,0:T(8,128)}, f32[1]{0:T(128)}) custom-call(f32[1,8192]{1,0:T(1,128)} %bitcast.6, s32[1,8192]{1,0:T(1,128)} %bitcast.7, s32[3,8192]{1,0:T(4,128)} %bitcast.5, f32[3,4,8192]{2,1,0:T(4,128)} %bitcast.4, f32[27,54,216]{2,1,0:T(8,128)} %bc_hbm.1, bf16[224,256]{1,0:T(8,128)(2,1)} %constant.14.clone.fx_hi, ...), custom_call_target="tpu_custom_call" | custom-call | tf_op jit(solution)/shard_map/energy/pallas_call | solution.py:371
  92.3 2.6 %copy.16 = f32[27,54,216]{2,1,0:T(8,128)} copy(f32[27,54,216]{2,1,0:T(8,128)} %get-tuple-element.4) | data formatting | bytes 2519424

commit v2 on v1

v2 whole, which is shorter than its diff:
```python
import functools
import math

import jax
import jax.numpy as jnp
import numpy as np
from jax import lax
from jax.experimental import pallas as pl
from jax.experimental.pallas import tpu as pltpu
from jax.sharding import PartitionSpec as P

MESH = pl.DeviceIdType.MESH
TAPS = 4
LANES = 128
NT_DIMS = (((1,), (1,)), ((), ()))


def round_up(value, unit):
    return -(-value // unit) * unit


def split_const(matrix):
    high = matrix.astype(jnp.bfloat16)
    low = (matrix - high.astype(np.float64)).astype(jnp.bfloat16)
    return high, low


def split_value(value):
    high = value.astype(jnp.bfloat16)
    low = (value - high.astype(jnp.float32)).astype(jnp.bfloat16)
    return high, low


def dot_f32(left, right):
    return jnp.dot(left, right, preferred_element_type=jnp.float32)


def dot_nt(left, right):
    return lax.dot_general(left, right, NT_DIMS, preferred_element_type=jnp.float32)


def encode(value, code_lane):
    lane = lax.broadcasted_iota(jnp.int32, (1, value.shape[1]), 1)
    top = jnp.max(jnp.abs(value), axis=1, keepdims=True)
    code = jnp.ceil(jnp.log2(jnp.maximum(top, 1e-35)) * 64.0) + 1.0
    steps = jnp.round(value * (jnp.exp2(code * (-1.0 / 64.0)) * 32766.0))
    return jnp.where(lane == code_lane, code, steps).astype(jnp.int32).astype(jnp.int16)


def decode(packed, code_lane):
    lane = lax.broadcasted_iota(jnp.int32, (1, packed.shape[1]), 1)
    steps = packed.astype(jnp.int32).astype(jnp.float32)
    code = steps[:, code_lane:code_lane + 1]
    return jnp.where(lane == code_lane, 0.0, steps * (jnp.exp2(code * (1.0 / 64.0)) * (1.0 / 32766.0)))


CODE = 15


def swap_lane_groups(arrays, unit):
    lane = lax.broadcasted_iota(jnp.int32, (1, LANES), 1)
    arrays = list(arrays)
    bit = len(arrays) // 2
    while bit:
        stays = (lane // (unit * bit)) % 2 == 0
        for low in range(len(arrays)):
            if low & bit == 0:
                a, b = arrays[low], arrays[low | bit]
                arrays[low] = jnp.where(stays, a, pltpu.roll(b, unit * bit, 1))
                arrays[low | bit] = jnp.where(stays, pltpu.roll(a, LANES - unit * bit, 1), b)
        bit //= 2
    return arrays


def energy_kernel(sizes, charge_hbm, mask_hbm, idx_hbm, w_hbm, bc_hbm, fx_hi, fx_lo, fy_hi, fy_lo, wz_hi, wz_lo, flip_hbm,
                  ek_ref, energy_ref,
                  charge_ref, mask_ref, idx_ref, w_ref, a_hi, a_lo, b_hi0, b_lo0, b_hi1, b_lo1, y_ref, z_ref, q_ref, wide_x,
                  bc_ref, fxh, fxl, fyh, fyl, wzh, wzl, flip_ref,
                  send_x, recv_x, send_y, recv_y, send_m, recv_m, send_r, recv_r, part, sums_y, part_z, sums_z,
                  sem_in, sem_sx, sem_rx, sem_sy, sem_ry, sem_sm, sem_rm, sem_row, sem_ey, sem_ez):
    grid_n, y_devs, z_devs, len_x, len_z, planes, rows_k, chunks, groups, chunk = sizes
    me_y = lax.axis_index('ydom')
    me_z = lax.axis_index('zdom')
    away_y = y_devs - 1 - me_y
    away_z = z_devs - 1 - me_z
    row_z = lax.rem(z_devs - me_z, z_devs)
    mirror = {'ydom': away_y, 'zdom': away_z}
    mirror_row = {'ydom': away_y, 'zdom': row_z}
    ring_y = [lax.rem(me_y + k, y_devs) for k in range(y_devs)]
    ring_z = [lax.rem(me_z + k, z_devs) for k in range(z_devs)]

    barrier = pltpu.get_barrier_semaphore()
    peers = [{'ydom': dest} for dest in ring_y[1:]] + [{'zdom': dest} for dest in ring_z[1:]] + [mirror, mirror_row]
    for peer in peers:
        pl.semaphore_signal(barrier, inc=1, device_id=peer, device_id_type=MESH)

    loads = [pltpu.make_async_copy(src, dst, sem_in.at[n]) for n, (src, dst) in enumerate(
        [(charge_hbm, charge_ref), (mask_hbm, mask_ref), (idx_hbm, idx_ref), (w_hbm, w_ref),
         (fx_hi, fxh), (fx_lo, fxl), (fy_hi, fyh), (fy_lo, fyl), (wz_hi, wzh), (wz_lo, wzl), (flip_hbm, flip_ref),
         (bc_hbm, bc_ref)])]
    for load in loads:
        load.start()

    def remote(src, dst, send_sem, recv_sem, peer):
        return pltpu.make_async_remote_copy(src_ref=src, dst_ref=dst, send_sem=send_sem, recv_sem=recv_sem,
                                            device_id=peer, device_id_type=MESH)

    lane = lax.broadcasted_iota(jnp.int32, (1, LANES), 1)
    is_real = (lane // 16) % 2 == 0
    per_dest = 4 * 32

    slots = charge_hbm.shape[1]
    n_chunks = slots // chunk
    rows_a = a_hi.shape[1]
    top_a = round_up(grid_n, 16)
    rows_y = b_hi0.shape[0] // 16
    for c in range(n_chunks):
        for ref in (a_hi, a_lo):
            ref[c, top_a:, :] = jnp.zeros((rows_a - top_a, chunk), jnp.bfloat16)

    def tap_block(row_id, positions, weights):
        value = jnp.where(row_id == positions[0], weights[0], 0.0)
        for tap in range(1, TAPS):
            value = jnp.where(row_id == positions[tap], weights[tap], value)
        return value

    def make_lines(c, carry):
        cols = pl.ds(pl.multiple_of(c * chunk, chunk), chunk)
        weight = charge_ref[:, cols] * mask_ref[:, cols].astype(jnp.float32)
        base = [idx_ref[d:d + 1, cols] for d in range(3)]
        taps = [[w_ref[d, s:s + 1, cols] for s in range(TAPS)] for d in range(3)]
        taps[0] = [tap * weight for tap in taps[0]]
        pos_x = [base[0] + s for s in range(TAPS)]
        pos_x = [jnp.where(pos >= grid_n, pos - grid_n, pos) for pos in pos_x]
        pos_y = [base[1] + s for s in range(TAPS)]
        pos_z = [base[2] + s for s in range(TAPS)]
        eight = lax.broadcasted_iota(jnp.int32, (8, chunk), 0)
        sixteen = lax.broadcasted_iota(jnp.int32, (16, chunk), 0)
        for row in range(0, y_ref.shape[1], 8):
            y_ref[c, row:row + 8, :] = tap_block(eight + row, pos_y, taps[1])
        for h, (first_z, n_z) in enumerate(groups):
            row_id = jnp.where(sixteen < n_z, sixteen + first_z, -1)
            z_ref[c, h * 16:(h + 1) * 16, :] = tap_block(row_id, pos_z, taps[2])
        for row in range(0, top_a, 16):
            high, low = split_value(tap_block(sixteen + row, pos_x, taps[0]))
            a_hi[c, row:row + 16, :] = high
            a_lo[c, row:row + 16, :] = low
        return carry

    def make_b(h, c, high_ref, low_ref):
        line_z = z_ref[c, pl.ds(pl.multiple_of(h * 16, 16), 16), :]
        for y in range(rows_y):
            high, low = split_value(y_ref[c, y:y + 1, :] * line_z)
            high_ref[y * 16:(y + 1) * 16, :] = high
            low_ref[y * 16:(y + 1) * 16, :] = low

    used = slice(0, rows_y * 16)

    def add_chunk(c, high_ref, low_ref):
        high, low = a_hi[c], a_lo[c]
        q_ref[used, :] += dot_nt(high_ref[...], high) + dot_nt(low_ref[...], high) + dot_nt(high_ref[...], low)

    sign_rows = z_devs * rows_k
    copies_x, copies_y = [], []

    def y_direction(h):
        for copy in copies_x[h]:
            copy.wait_recv()
        def two_rows_of_planes(p, carry):
            cols = []
            for n in range(2):
                lines = pl.ds(pl.multiple_of(p * 64 + n * 32, 32), 32)
                cols.append(jnp.concatenate([decode(recv_x[h, s, lines, :], CODE) for s in range(y_devs)], axis=0))
            high, low = split_value(jnp.concatenate(cols, axis=1))
            block = dot_f32(fyh[...], high) + dot_f32(fyl[...], high) + dot_f32(fyh[...], low)
            values = []
            for n in range(2):
                cos_part = block[:sign_rows, n * LANES:(n + 1) * LANES]
                sin_part = block[sign_rows:, n * LANES:(n + 1) * LANES]
                values.append(cos_part + jnp.where(is_real, pltpu.roll(sin_part, LANES - 16, 1),
                                                   -pltpu.roll(sin_part, 16, 1)))
            for dest in range(z_devs):
                rows = slice(dest * rows_k, (dest + 1) * rows_k)
                both = jnp.concatenate([values[0][rows], values[1][rows]], axis=0)
                send_y[dest, h, pl.ds(pl.multiple_of(p * 2 * rows_k, 16), 2 * rows_k), :] = encode(both, CODE)
            return carry

        lax.fori_loop(0, 2, two_rows_of_planes, 0)
        group = []
        for k in range(1, z_devs):
            copy = remote(send_y.at[ring_z[k], h], recv_y.at[me_z, h], sem_sy.at[h, k], sem_ry.at[h, k],
                          {'zdom': ring_z[k]})
            copy.start()
            group.append(copy)
        copies_y.append(group)
        recv_y[me_z, h] = send_y[me_z, h]

    for load in loads[:4]:
        load.wait()
    lax.fori_loop(0, n_chunks, make_lines, 0)
    make_b(0, 0, b_hi0, b_lo0)
    for h in range(len(groups)):
        q_ref[...] = jnp.zeros_like(q_ref)

        def pair(step, carry, h=h):
            after = 2 * step + 2
            wrap = after // n_chunks
            after_c = after - wrap * n_chunks
            make_b(h, 2 * step + 1, b_hi1, b_lo1)
            add_chunk(2 * step, b_hi0, b_lo0)
            make_b(h + wrap, after_c, b_hi0, b_lo0)
            add_chunk(2 * step + 1, b_hi1, b_lo1)
            return carry

        lax.fori_loop(0, n_chunks // 2, pair, 0)

        if h == 0:
            for load in loads[4:]:
                load.wait()
        for half in range(2):
            high, low = split_value(q_ref[half * 256:(half + 1) * 256, :])
            block = dot_nt(fxh[...], high) + dot_nt(fxl[...], high) + dot_nt(fxh[...], low)
            for tile in range(2):
                lanes = slice(tile * LANES, (tile + 1) * LANES)
                by_y = swap_lane_groups([block[b * 32:(b + 1) * 32, lanes] for b in range(8)], 16)
                for y in range(8):
                    wide_x[pl.ds((half * 2 + tile) * 8 + y, 4 * y_devs, stride=40), :] = by_y[y]

        def pack_rows(dest, carry, h=h):
            for tq in range(4):
                rows = pl.ds(pl.multiple_of((dest * 4 + tq) * 40, 8), 32)
                send_x[h, pl.ds(pl.multiple_of(dest * per_dest + tq * 32, 32), 32), :] = encode(wide_x[rows, :], CODE)
            return carry

        lax.fori_loop(0, y_devs, pack_rows, 0)
        if h == 0:
            pl.semaphore_wait(barrier, len(peers))
        group = []
        for k in range(1, y_devs):
            start = pl.multiple_of(ring_y[k] * per_dest, 16)
            copy = remote(send_x.at[h, pl.ds(start, per_dest), :], recv_x.at[h, me_y],
                          sem_sx.at[h, k], sem_rx.at[h, k], {'ydom': ring_y[k]})
            copy.start()
            group.append(copy)
        copies_x.append(group)
        recv_x[h, me_y] = send_x[h, pl.ds(pl.multiple_of(me_y * per_dest, 16), per_dest), :]
        if h >= 1:
            y_direction(h - 1)
    y_direction(len(groups) - 1)

    width = wzh.shape[1] // 2
    total = jnp.zeros((len_z, grid_n), jnp.float32)
    send_r[...] = jnp.zeros_like(send_r)
    copies_m = []
    for copy in [copy for group in copies_y for copy in group]:
        copy.wait_recv()
    real_wide = jnp.concatenate([is_real] * z_devs, axis=1)
    for c, (first, last) in enumerate(chunks):
        rows = slice(first * rows_k, last * rows_k)
        if c % 2 == 0:
            lines = slice(c * rows_k, (c + 2) * rows_k)
            by_plane = [swap_lane_groups([decode(recv_y[s, h, lines, :], CODE) for h in range(4)], 32)
                        for s in range(z_devs)]
        at = slice((c % 2) * rows_k, (c % 2 + 1) * rows_k)
        high, low = split_value(jnp.concatenate(
            [jnp.concatenate([by_plane[s][n][at] for s in range(z_devs)], axis=1) for n in range(last - first)], axis=0))
        nil = jnp.zeros_like(high)
        from_real, from_imag = [
            dot_f32(h, wzh[...]) + dot_f32(l, wzh[...]) + dot_f32(h, wzl[...])
            for h, l in ((jnp.where(real_wide, high, nil), jnp.where(real_wide, low, nil)),
                         (jnp.where(real_wide, nil, high), jnp.where(real_wide, nil, low)))]
        both_signs = [from_real + from_imag, from_real - from_imag]
        power, power_rev = [v[:, :width] * v[:, :width] + v[:, width:] * v[:, width:] for v in both_signs]
        for p in range(first, last, 2):
            both = []
            for kx in (p, p + 1):
                at = (kx - first) * rows_k
                value = 0.5 * bc_ref[kx] * power[at:at + len_z, :grid_n]
                ek_ref[kx] = value
                total = total + value
                high, low = split_value(power_rev[at:at + rows_k, :])
                flipped = dot_f32(flip_ref[...], high) + dot_f32(flip_ref[...], low)
                send_r[kx:kx + 1, :] = flipped[0:1, :]
                both.append(flipped)
            send_m[p * rows_k:(p + 2) * rows_k, :] = encode(jnp.concatenate(both, axis=0), width - 1)
        copy = remote(send_m.at[rows, :], recv_m.at[rows, :], sem_sm.at[c], sem_rm.at[c], mirror)
        copy.start()
        copies_m.append(copy)
    copy_row = remote(send_r, recv_r, sem_row.at[0], sem_row.at[1], mirror_row)
    copy_row.start()

    copy_row.wait_recv()
    is_first = lax.broadcasted_iota(jnp.int32, (len_z, grid_n), 0) == 0
    for c, (first, last) in enumerate(chunks):
        copies_m[c].wait_recv()
        for p in range(first, last, 2):
            both = decode(recv_m[p * rows_k:(p + 2) * rows_k, :], width - 1)
            for kx in (p, p + 1):
                if kx >= 1:
                    plane = len_x - kx
                    at = (kx - p) * rows_k
                    power = jnp.where(is_first, recv_r[kx:kx + 1, :grid_n], both[at:at + len_z, :grid_n])
                    value = 0.5 * bc_ref[plane] * power
                    ek_ref[plane] = value
                    total = total + value

    def spread_sum(value, out, sums, sems, axis, ring, me):
        out[...] = jnp.zeros_like(out) + value
        copies = []
        for k in range(1, len(ring)):
            copy = remote(out, sums.at[me], sems.at[0, k], sems.at[1, k], {axis: ring[k]})
            copy.start()
            copies.append(copy)
        sums[me] = jnp.zeros(out.shape, jnp.float32) + value
        for copy in copies:
            copy.wait_recv()
        result = sums[0]
        for s in range(1, len(ring)):
            result = result + sums[s]
        return result, copies

    local = jnp.sum(total, keepdims=True)
    over_z, copies_ez = spread_sum(local, part, sums_z, sem_ez, 'zdom', ring_z, me_z)
    over_all, copies_ey = spread_sum(over_z, part_z, sums_y, sem_ey, 'ydom', ring_y, me_y)
    energy_ref[0] = over_all[0, 0] / (grid_n * grid_n * grid_n)

    for copy in [x for g in copies_x + copies_y for x in g] + copies_m + [copy_row] + copies_ez + copies_ey:
        copy.wait_send()


def transforms(grid_n, y_devs, z_devs, len_x, len_y, len_z, planes, rows_k, groups):
    unit = 2.0 * math.pi / grid_n

    def angle(freq, pos):
        return ((freq[:, None] * pos[None, :]) % grid_n) * unit

    plane = np.arange(4)[None, None, :] * 4 + np.arange(4)[:, None, None]
    freq = (np.arange(y_devs)[None, :, None] * len_x + plane).reshape(-1)
    keep = np.broadcast_to(plane < planes, (4, y_devs, 4)).reshape(-1)
    phase = angle(freq, np.arange(grid_n))
    mat_x = np.zeros((4, 2, y_devs * 4, round_up(grid_n, LANES)))
    mat_x[:, 0, :, :grid_n] = (np.cos(phase) * keep[:, None]).reshape(4, y_devs * 4, grid_n)
    mat_x[:, 1, :, :grid_n] = (-np.sin(phase) * keep[:, None]).reshape(4, y_devs * 4, grid_n)
    mat_x = mat_x.reshape(8 * y_devs * 4, -1)
    pos = (np.arange(y_devs)[:, None] * len_y + np.arange(32)[None, :]).reshape(-1)
    used = np.tile(np.arange(32) < len_y + TAPS - 1, y_devs)
    ky = (np.arange(z_devs)[:, None] * len_z + np.arange(rows_k)[None, :]).reshape(-1)
    keep = np.tile(np.arange(rows_k) < len_z, z_devs)
    phase = angle(ky, pos)
    mask = keep[:, None] * used[None, :]
    mat_y = np.concatenate([np.cos(phase) * mask, np.sin(phase) * mask])
    width = round_up(grid_n, LANES)
    mat_z = np.zeros((z_devs, len(groups), 2, 16, 2, width))
    for dev in range(z_devs):
        for h, (first_z, n_z) in enumerate(groups):
            phase = angle(dev * len_z + first_z + np.arange(n_z), np.arange(grid_n))
            mat_z[dev, h, 0, :n_z, 0, :grid_n] = np.cos(phase)
            mat_z[dev, h, 1, :n_z, 0, :grid_n] = np.sin(phase)
            mat_z[dev, h, 0, :n_z, 1, :grid_n] = -np.sin(phase)
            mat_z[dev, h, 1, :n_z, 1, :grid_n] = np.cos(phase)
    mat_z = mat_z.reshape(z_devs * 128, 2 * width)
    flip = np.zeros((rows_k, rows_k))
    flip[0, 0] = 1.0
    flip[np.arange(1, len_z), len_z - np.arange(1, len_z)] = 1.0
    return (*split_const(mat_x), *split_const(mat_y), *split_const(mat_z), flip.astype(jnp.bfloat16))


def solution(mesh):
    y_devs = mesh.shape['ydom']
    z_devs = mesh.shape['zdom']
    slot_spec = P(('sys', 'ydom', 'zdom'))
    mode_spec = P(('sys', 'ydom'), 'zdom', None)

    def local_energy(charge, real_mask, grid_idx, spline_w, influence):
        len_x, len_k, grid_n = influence.shape
        len_y = grid_n // y_devs
        len_z = grid_n // z_devs
        slots = charge.shape[0]
        chunk = 1024
        rows_y = len_y + TAPS - 1
        rows_z = len_z + TAPS - 1
        cuts = [-(-rows_z * h // 4) for h in range(5)]
        groups = tuple((cuts[h], cuts[h + 1] - cuts[h]) for h in range(4))
        width = round_up(grid_n, LANES)
        planes = (len_x + 1) // 2
        rows_k = round_up(len_k, 8)
        chunks = tuple((p, min(p + 4, planes)) for p in range(0, planes, 4))
        sizes = (grid_n, y_devs, z_devs, len_x, len_z, planes, rows_k, chunks, groups, chunk)
        mats = transforms(grid_n, y_devs, z_devs, len_x, len_y, len_z, planes, rows_k, groups)
        f32, bf16, i16 = jnp.float32, jnp.bfloat16, jnp.int16
        vmem = pl.BlockSpec(memory_space=pltpu.VMEM)
        hbm = pl.BlockSpec(memory_space=pltpu.HBM)
        n, n_g, n_c = len(chunks), len(groups), slots // chunk
        dma = pltpu.SemaphoreType.DMA
        mode_energy, energy = pl.pallas_call(
            functools.partial(energy_kernel, sizes),
            name='energy',
            out_shape=(jax.ShapeDtypeStruct(influence.shape, f32), jax.ShapeDtypeStruct((1,), f32)),
            in_specs=[hbm] * (5 + len(mats)),
            out_specs=(vmem, pl.BlockSpec(memory_space=pltpu.SMEM)),
            scratch_shapes=[
                pltpu.VMEM((1, slots), f32), pltpu.VMEM((1, slots), jnp.int32), pltpu.VMEM((3, slots), jnp.int32),
                pltpu.VMEM((3, TAPS, slots), f32),
                pltpu.VMEM((n_c, width, chunk), bf16), pltpu.VMEM((n_c, width, chunk), bf16),
                *[pltpu.VMEM((rows_y * 16, chunk), bf16)] * 4,
                pltpu.VMEM((n_c, 32, chunk), f32), pltpu.VMEM((n_c, 16 * n_g + 16, chunk), f32),
                pltpu.VMEM((512, width), f32), pltpu.VMEM((y_devs * 4 * 40, LANES), f32),
                pltpu.VMEM(influence.shape, f32), *[pltpu.VMEM(mat.shape, mat.dtype) for mat in mats],
                pltpu.VMEM((n_g, y_devs * 128, LANES), i16),
                pltpu.VMEM((n_g, y_devs, 128, LANES), i16),
                pltpu.VMEM((z_devs, n_g, 4 * rows_k, LANES), i16),
                pltpu.VMEM((z_devs, n_g, 4 * rows_k, LANES), i16),
                pltpu.VMEM((planes * rows_k, width), i16),
                pltpu.VMEM((planes * rows_k, width), i16),
                pltpu.VMEM((round_up(planes, 8), width), f32),
                pltpu.VMEM((round_up(planes, 8), width), f32),
                pltpu.VMEM((8, LANES), f32),
                pltpu.VMEM((y_devs, 8, LANES), f32),
                pltpu.VMEM((8, LANES), f32),
                pltpu.VMEM((z_devs, 8, LANES), f32),
                dma((12,)), dma((n_g, y_devs)), dma((n_g, y_devs)), dma((n_g, z_devs)), dma((n_g, z_devs)),
                dma((n,)), dma((n,)), dma((2,)), dma((2, y_devs)), dma((2, z_devs)),
            ],
            compiler_params=pltpu.CompilerParams(collective_id=0, has_side_effects=True,
                                                 vmem_limit_bytes=60 * 2**20),
        )(charge.reshape(1, slots), real_mask.reshape(1, slots), grid_idx.T, jnp.transpose(spline_w, (1, 2, 0)),
          influence, *mats)
        return mode_energy, energy

    return jax.shard_map(local_energy, mesh=mesh, in_specs=(slot_spec, slot_spec, P(('sys', 'ydom', 'zdom'), None), P(('sys', 'ydom', 'zdom'), None, None), mode_spec), out_specs=(mode_spec, P('sys')), check_vma=False)
```

time: 96.8 us -> 90.9 us (0.939)
  Pallas kernels: 91.7 us -> 85.8 us
    pallas_call x1, Pallas kernels: 91.7 us -> 85.8 us  [local_energy(): pl.pallas_call(functools.partial(energy_kernel, sizes), name='energy', ou...]
where the time goes in v2:
time: 90.9 us; the launch traced here: 90.8 us
  Pallas kernels  85.8 us (94%)
  local copies, waits for them, and re-layouts  2.63 us (3%)
  between operations  2.37 us (3%)
    pallas_call x1, Pallas kernels, local_energy(): pl.pallas_call(functools.partial(energy_kernel, sizes), name='energy', ou...  85.8 us
    unnamed x1, local copies, waits for them, and re-layouts  2.63 us

profile of v2, /device:TPU:97, one launch (start us, length us, event | category | flops | bytes accessed | tf_op | source)
XLA Modules:
  0.0 90.8 jit_solution(13913807333455402713)
XLA Ops:
  0.6 85.8 %energy.1 = (f32[27,54,216]{2,1,0:T(8,128)}, f32[1]{0:T(128)}) custom-call(f32[1,8192]{1,0:T(1,128)} %bitcast.6, s32[1,8192]{1,0:T(1,128)} %bitcast.7, s32[3,8192]{1,0:T(4,128)} %bitcast.5, f32[3,4,8192]{2,1,0:T(4,128)} %bitcast.4, f32[27,54,216]{2,1,0:T(8,128)} %bc_hbm.1, bf16[256,256]{1,0:T(8,128)(2,1)} %constant.14.clone.fx_hi, ...), custom_call_target="tpu_custom_call" | custom-call | tf_op jit(solution)/shard_map/energy/pallas_call | solution.py:395
  86.4 2.6 %copy.16 = f32[27,54,216]{2,1,0:T(8,128)} copy(f32[27,54,216]{2,1,0:T(8,128)} %get-tuple-element.4) | data formatting | bytes 2519424

commit v3 on v2

--- a/solution.py
+++ b/solution.py
@@ -76,8 +76,8 @@
                   ek_ref, energy_ref,
                   charge_ref, mask_ref, idx_ref, w_ref, a_hi, a_lo, b_hi0, b_lo0, b_hi1, b_lo1, y_ref, z_ref, q_ref, wide_x,
                   bc_ref, fxh, fxl, fyh, fyl, wzh, wzl, flip_ref,
-                  send_x, recv_x, send_y, recv_y, send_m, recv_m, send_r, recv_r, part, sums_y, part_z, sums_z,
-                  sem_in, sem_sx, sem_rx, sem_sy, sem_ry, sem_sm, sem_rm, sem_row, sem_ey, sem_ez):
+                  send_x, recv_x, send_y, recv_y, send_m, recv_m, send_r, recv_r, bc_mirror, bc_row, wide_m, part, sums_y, part_z, sums_z,
+                  sem_in, sem_sx, sem_rx, sem_sy, sem_ry, sem_sm, sem_rm, sem_row, sem_ey, sem_ez, sem_bc):
     grid_n, y_devs, z_devs, len_x, len_z, planes, rows_k, chunks, groups, chunk = sizes
     me_y = lax.axis_index('ydom')
     me_z = lax.axis_index('zdom')
@@ -161,43 +161,57 @@
         q_ref[used, :] += dot_nt(high_ref[...], high) + dot_nt(low_ref[...], high) + dot_nt(high_ref[...], low)
 
     sign_rows = z_devs * rows_k
-    copies_x, copies_y = [], []
+
+    def y_half(h, p):
+        cols = []
+        for n in range(2):
+            lines = pl.ds(pl.multiple_of(p * 64 + n * 32, 32), 32)
+            cols.append(jnp.concatenate([decode(recv_x[h, s, lines, :], CODE) for s in range(y_devs)], axis=0))
+        high, low = split_value(jnp.concatenate(cols, axis=1))
+        block = dot_f32(fyh[...], high) + dot_f32(fyl[...], high) + dot_f32(fyh[...], low)
+        values = []
+        for n in range(2):
+            cos_part = block[:sign_rows, n * LANES:(n + 1) * LANES]
+            sin_part = block[sign_rows:, n * LANES:(n + 1) * LANES]
+            values.append(cos_part + jnp.where(is_real, pltpu.roll(sin_part, LANES - 16, 1),
+                                               -pltpu.roll(sin_part, 16, 1)))
+        for dest in range(z_devs):
+            rows = slice(dest * rows_k, (dest + 1) * rows_k)
+            both = jnp.concatenate([values[0][rows], values[1][rows]], axis=0)
+            send_y[dest, h, pl.ds(pl.multiple_of(p * 2 * rows_k, 16), 2 * rows_k), :] = encode(both, CODE)
+
+    def x_copy(h, p, k):
+        start = pl.multiple_of(ring_y[k] * per_dest + p * 64, 64)
+        return remote(send_x.at[h, pl.ds(start, 64), :], recv_x.at[h, me_y, pl.ds(pl.multiple_of(p * 64, 64), 64), :],
+                      sem_sx.at[2 * h + p, k], sem_rx.at[2 * h + p, k], {'ydom': ring_y[k]})
+
+    def y_copy(h, p, k):
+        rows = pl.ds(pl.multiple_of(p * 2 * rows_k, 16), 2 * rows_k)
+        return remote(send_y.at[ring_z[k], h, rows, :], recv_y.at[me_z, h, rows, :],
+                      sem_sy.at[2 * h + p, k], sem_ry.at[2 * h + p, k], {'zdom': ring_z[k]})
 
     def y_direction(h):
-        for copy in copies_x[h]:
-            copy.wait_recv()
-        def two_rows_of_planes(p, carry):
-            cols = []
-            for n in range(2):
-                lines = pl.ds(pl.multiple_of(p * 64 + n * 32, 32), 32)
-                cols.append(jnp.concatenate([decode(recv_x[h, s, lines, :], CODE) for s in range(y_devs)], axis=0))
-            high, low = split_value(jnp.concatenate(cols, axis=1))
-            block = dot_f32(fyh[...], high) + dot_f32(fyl[...], high) + dot_f32(fyh[...], low)
-            values = []
-            for n in range(2):
-                cos_part = block[:sign_rows, n * LANES:(n + 1) * LANES]
-                sin_part = block[sign_rows:, n * LANES:(n + 1) * LANES]
-                values.append(cos_part + jnp.where(is_real, pltpu.roll(sin_part, LANES - 16, 1),
-                                                   -pltpu.roll(sin_part, 16, 1)))
-            for dest in range(z_devs):
-                rows = slice(dest * rows_k, (dest + 1) * rows_k)
-                both = jnp.concatenate([values[0][rows], values[1][rows]], axis=0)
-                send_y[dest, h, pl.ds(pl.multiple_of(p * 2 * rows_k, 16), 2 * rows_k), :] = encode(both, CODE)
+        def one_half(p, carry):
+            for k in range(1, y_devs):
+                x_copy(h, p, k).wait_recv()
+            y_half(h, p)
+            for k in range(1, z_devs):
+                y_copy(h, p, k).start()
+            rows = pl.ds(pl.multiple_of(p * 2 * rows_k, 16), 2 * rows_k)
+            recv_y[me_z, h, rows, :] = send_y[me_z, h, rows, :]
             return carry
 
-        lax.fori_loop(0, 2, two_rows_of_planes, 0)
-        group = []
-        for k in range(1, z_devs):
-            copy = remote(send_y.at[ring_z[k], h], recv_y.at[me_z, h], sem_sy.at[h, k], sem_ry.at[h, k],
-                          {'zdom': ring_z[k]})
-            copy.start()
-            group.append(copy)
-        copies_y.append(group)
-        recv_y[me_z, h] = send_y[me_z, h]
+        lax.fori_loop(0, 2, one_half, 0)
 
     for load in loads[:4]:
         load.wait()
     lax.fori_loop(0, n_chunks, make_lines, 0)
+    pl.semaphore_wait(barrier, len(peers))
+    upper = pl.ds(planes, len_x - planes)
+    copies_bc = [remote(bc_hbm.at[upper], bc_mirror, sem_bc.at[0, 0], sem_bc.at[1, 0], mirror),
+                 remote(bc_hbm.at[upper, pl.ds(0, 8), :], bc_row, sem_bc.at[0, 1], sem_bc.at[1, 1], mirror_row)]
+    for copy in copies_bc:
+        copy.start()
     make_b(0, 0, b_hi0, b_lo0)
     for h in range(len(groups)):
         q_ref[...] = jnp.zeros_like(q_ref)
@@ -233,16 +247,9 @@
             return carry
 
         lax.fori_loop(0, y_devs, pack_rows, 0)
-        if h == 0:
-            pl.semaphore_wait(barrier, len(peers))
-        group = []
-        for k in range(1, y_devs):
-            start = pl.multiple_of(ring_y[k] * per_dest, 16)
-            copy = remote(send_x.at[h, pl.ds(start, per_dest), :], recv_x.at[h, me_y],
-                          sem_sx.at[h, k], sem_rx.at[h, k], {'ydom': ring_y[k]})
-            copy.start()
-            group.append(copy)
-        copies_x.append(group)
+        for p in range(2):
+            for k in range(1, y_devs):
+                x_copy(h, p, k).start()
         recv_x[h, me_y] = send_x[h, pl.ds(pl.multiple_of(me_y * per_dest, 16), per_dest), :]
         if h >= 1:
             y_direction(h - 1)
@@ -250,14 +257,19 @@
 
     width = wzh.shape[1] // 2
     total = jnp.zeros((len_z, grid_n), jnp.float32)
+    is_first = lax.broadcasted_iota(jnp.int32, (len_z, grid_n), 0) == 0
+    for copy in copies_bc:
+        copy.wait_recv()
     send_r[...] = jnp.zeros_like(send_r)
+    wide_m[...] = jnp.zeros_like(wide_m)
     copies_m = []
-    for copy in [copy for group in copies_y for copy in group]:
-        copy.wait_recv()
     real_wide = jnp.concatenate([is_real] * z_devs, axis=1)
     for c, (first, last) in enumerate(chunks):
         rows = slice(first * rows_k, last * rows_k)
         if c % 2 == 0:
+            for h in range(len(groups)):
+                for k in range(1, z_devs):
+                    y_copy(h, c // 2, k).wait_recv()
             lines = slice(c * rows_k, (c + 2) * rows_k)
             by_plane = [swap_lane_groups([decode(recv_y[s, h, lines, :], CODE) for h in range(4)], 32)
                         for s in range(z_devs)]
@@ -272,7 +284,6 @@
         both_signs = [from_real + from_imag, from_real - from_imag]
         power, power_rev = [v[:, :width] * v[:, :width] + v[:, width:] * v[:, width:] for v in both_signs]
         for p in range(first, last, 2):
-            both = []
             for kx in (p, p + 1):
                 at = (kx - first) * rows_k
                 value = 0.5 * bc_ref[kx] * power[at:at + len_z, :grid_n]
@@ -280,31 +291,21 @@
                 total = total + value
                 high, low = split_value(power_rev[at:at + rows_k, :])
                 flipped = dot_f32(flip_ref[...], high) + dot_f32(flip_ref[...], low)
-                send_r[kx:kx + 1, :] = flipped[0:1, :]
-                both.append(flipped)
-            send_m[p * rows_k:(p + 2) * rows_k, :] = encode(jnp.concatenate(both, axis=0), width - 1)
+                if kx >= 1:
+                    plane = len_x - kx - planes
+                    factor = jnp.where(is_first, bc_row[plane, 0:1, :], bc_mirror[plane])
+                    value = 0.5 * factor * flipped[:len_z, :grid_n]
+                    total = total + value
+                    send_r[kx:kx + 1, :grid_n] = value[0:1, :]
+                    wide_m[(kx - p) * rows_k:(kx - p) * rows_k + len_z, :grid_n] = value
+            send_m[p * rows_k:(p + 2) * rows_k, :] = encode(wide_m[...], width - 1)
         copy = remote(send_m.at[rows, :], recv_m.at[rows, :], sem_sm.at[c], sem_rm.at[c], mirror)
         copy.start()
         copies_m.append(copy)
     copy_row = remote(send_r, recv_r, sem_row.at[0], sem_row.at[1], mirror_row)
     copy_row.start()
 
-    copy_row.wait_recv()
-    is_first = lax.broadcasted_iota(jnp.int32, (len_z, grid_n), 0) == 0
-    for c, (first, last) in enumerate(chunks):
-        copies_m[c].wait_recv()
-        for p in range(first, last, 2):
-            both = decode(recv_m[p * rows_k:(p + 2) * rows_k, :], width - 1)
-            for kx in (p, p + 1):
-                if kx >= 1:
-                    plane = len_x - kx
-                    at = (kx - p) * rows_k
-                    power = jnp.where(is_first, recv_r[kx:kx + 1, :grid_n], both[at:at + len_z, :grid_n])
-                    value = 0.5 * bc_ref[plane] * power
-                    ek_ref[plane] = value
-                    total = total + value
-
-    def spread_sum(value, out, sums, sems, axis, ring, me):
+    def start_sum(value, out, sums, sems, axis, ring, me):
         out[...] = jnp.zeros_like(out) + value
         copies = []
         for k in range(1, len(ring)):
@@ -312,20 +313,39 @@
             copy.start()
             copies.append(copy)
         sums[me] = jnp.zeros(out.shape, jnp.float32) + value
+        return copies
+
+    def end_sum(sums, copies):
         for copy in copies:
             copy.wait_recv()
         result = sums[0]
-        for s in range(1, len(ring)):
+        for s in range(1, len(copies) + 1):
             result = result + sums[s]
-        return result, copies
-
-    local = jnp.sum(total, keepdims=True)
-    over_z, copies_ez = spread_sum(local, part, sums_z, sem_ez, 'zdom', ring_z, me_z)
-    over_all, copies_ey = spread_sum(over_z, part_z, sums_y, sem_ey, 'ydom', ring_y, me_y)
-    energy_ref[0] = over_all[0, 0] / (grid_n * grid_n * grid_n)
-
-    for copy in [x for g in copies_x + copies_y for x in g] + copies_m + [copy_row] + copies_ez + copies_ey:
+        return result
+
+    copies_ez = start_sum(jnp.sum(total, keepdims=True), part, sums_z, sem_ez, 'zdom', ring_z, me_z)
+    copies_ey = start_sum(end_sum(sums_z, copies_ez), part_z, sums_y, sem_ey, 'ydom', ring_y, me_y)
+
+    copy_row.wait_recv()
+    for c, (first, last) in enumerate(chunks):
+        copies_m[c].wait_recv()
+        for p in range(first, last, 2):
+            both = decode(recv_m[p * rows_k:(p + 2) * rows_k, :], width - 1)
+            for kx in (p, p + 1):
+                if kx >= 1:
+                    at = (kx - p) * rows_k
+                    ek_ref[len_x - kx] = jnp.where(is_first, recv_r[kx:kx + 1, :grid_n], both[at:at + len_z, :grid_n])
+
+    energy_ref[0] = end_sum(sums_y, copies_ey)[0, 0] / (grid_n * grid_n * grid_n)
+
+    for copy in copies_m + [copy_row] + copies_ez + copies_ey + copies_bc:
         copy.wait_send()
+    for h in range(len(groups)):
+        for p in range(2):
+            for k in range(1, y_devs):
+                x_copy(h, p, k).wait_send()
+            for k in range(1, z_devs):
+                y_copy(h, p, k).wait_send()
 
 
 def transforms(grid_n, y_devs, z_devs, len_x, len_y, len_z, planes, rows_k, groups):
@@ -414,12 +434,15 @@
                 pltpu.VMEM((planes * rows_k, width), i16),
                 pltpu.VMEM((round_up(planes, 8), width), f32),
                 pltpu.VMEM((round_up(planes, 8), width), f32),
+                pltpu.VMEM((len_x - planes, len_k, grid_n), f32),
+                pltpu.VMEM((len_x - planes, 8, grid_n), f32),
+                pltpu.VMEM((2 * rows_k, width), f32),
                 pltpu.VMEM((8, LANES), f32),
                 pltpu.VMEM((y_devs, 8, LANES), f32),
                 pltpu.VMEM((8, LANES), f32),
                 pltpu.VMEM((z_devs, 8, LANES), f32),
-                dma((12,)), dma((n_g, y_devs)), dma((n_g, y_devs)), dma((n_g, z_devs)), dma((n_g, z_devs)),
-                dma((n,)), dma((n,)), dma((2,)), dma((2, y_devs)), dma((2, z_devs)),
+                dma((12,)), dma((2 * n_g, y_devs)), dma((2 * n_g, y_devs)), dma((2 * n_g, z_devs)), dma((2 * n_g, z_devs)),
+                dma((n,)), dma((n,)), dma((2,)), dma((2, y_devs)), dma((2, z_devs)), dma((2, 2)),
             ],
             compiler_params=pltpu.CompilerParams(collective_id=0, has_side_effects=True,
                                                  vmem_limit_bytes=60 * 2**20),

time: 90.9 us -> 90.1 us (level)
  no operation moved by 1% of the time
where the time goes in v3:
time: 90.1 us; the launch traced here: 90 us
  Pallas kernels  85 us (94%)
  local copies, waits for them, and re-layouts  2.63 us (3%)
  between operations  2.37 us (3%)
    pallas_call x1, Pallas kernels, local_energy(): pl.pallas_call(functools.partial(energy_kernel, sizes), name='energy', ou...  85 us
    unnamed x1, local copies, waits for them, and re-layouts  2.63 us

profile of v3, /device:TPU:97, one launch (start us, length us, event | category | flops | bytes accessed | tf_op | source)
XLA Modules:
  0.0 90.0 jit_solution(687750802232532586)
XLA Ops:
  0.6 85.0 %energy.1 = (f32[27,54,216]{2,1,0:T(8,128)}, f32[1]{0:T(128)}) custom-call(f32[1,8192]{1,0:T(1,128)} %bitcast.6, s32[1,8192]{1,0:T(1,128)} %bitcast.7, s32[3,8192]{1,0:T(4,128)} %bitcast.5, f32[3,4,8192]{2,1,0:T(4,128)} %bitcast.4, f32[27,54,216]{2,1,0:T(8,128)} %bc_hbm.1, bf16[256,256]{1,0:T(8,128)(2,1)} %constant.14.clone.fx_hi, ...), custom_call_target="tpu_custom_call" | custom-call | tf_op jit(solution)/shard_map/energy/pallas_call | solution.py:415
  85.6 2.6 %copy.16 = f32[27,54,216]{2,1,0:T(8,128)} copy(f32[27,54,216]{2,1,0:T(8,128)} %get-tuple-element.4) | data formatting | bytes 2519424

commit v4 on v3

--- a/solution.py
+++ b/solution.py
@@ -156,9 +156,9 @@
 
     used = slice(0, rows_y * 16)
 
-    def add_chunk(c, high_ref, low_ref):
+    def add_chunk(slot, c, high_ref, low_ref):
         high, low = a_hi[c], a_lo[c]
-        q_ref[used, :] += dot_nt(high_ref[...], high) + dot_nt(low_ref[...], high) + dot_nt(high_ref[...], low)
+        q_ref[slot, used, :] += dot_nt(high_ref[...], high) + dot_nt(low_ref[...], high) + dot_nt(high_ref[...], low)
 
     sign_rows = z_devs * rows_k
 
@@ -205,34 +205,42 @@
 
     for load in loads[:4]:
         load.wait()
-    lax.fori_loop(0, n_chunks, make_lines, 0)
     pl.semaphore_wait(barrier, len(peers))
     upper = pl.ds(planes, len_x - planes)
     copies_bc = [remote(bc_hbm.at[upper], bc_mirror, sem_bc.at[0, 0], sem_bc.at[1, 0], mirror),
                  remote(bc_hbm.at[upper, pl.ds(0, 8), :], bc_row, sem_bc.at[0, 1], sem_bc.at[1, 1], mirror_row)]
     for copy in copies_bc:
         copy.start()
-    make_b(0, 0, b_hi0, b_lo0)
-    for h in range(len(groups)):
-        q_ref[...] = jnp.zeros_like(q_ref)
-
-        def pair(step, carry, h=h):
+    q_ref[...] = jnp.zeros_like(q_ref)
+
+    def first_two(c, carry):
+        make_lines(c, 0)
+        make_b(0, c, b_hi0, b_lo0)
+        add_chunk(0, c, b_hi0, b_lo0)
+        make_b(1, c, b_hi1, b_lo1)
+        add_chunk(1, c, b_hi1, b_lo1)
+        return carry
+
+    def one_more(h):
+        slot = h % 2
+        q_ref[slot] = jnp.zeros(q_ref.shape[1:], jnp.float32)
+
+        def pair(step, carry):
             after = 2 * step + 2
             wrap = after // n_chunks
             after_c = after - wrap * n_chunks
             make_b(h, 2 * step + 1, b_hi1, b_lo1)
-            add_chunk(2 * step, b_hi0, b_lo0)
+            add_chunk(slot, 2 * step, b_hi0, b_lo0)
             make_b(h + wrap, after_c, b_hi0, b_lo0)
-            add_chunk(2 * step + 1, b_hi1, b_lo1)
+            add_chunk(slot, 2 * step + 1, b_hi1, b_lo1)
             return carry
 
         lax.fori_loop(0, n_chunks // 2, pair, 0)
 
-        if h == 0:
-            for load in loads[4:]:
-                load.wait()
+    def x_direction(h):
+        slot = h % 2
         for half in range(2):
-            high, low = split_value(q_ref[half * 256:(half + 1) * 256, :])
+            high, low = split_value(q_ref[slot, half * 256:(half + 1) * 256, :])
             block = dot_nt(fxh[...], high) + dot_nt(fxl[...], high) + dot_nt(fxh[...], low)
             for tile in range(2):
                 lanes = slice(tile * LANES, (tile + 1) * LANES)
@@ -251,9 +259,21 @@
             for k in range(1, y_devs):
                 x_copy(h, p, k).start()
         recv_x[h, me_y] = send_x[h, pl.ds(pl.multiple_of(me_y * per_dest, 16), per_dest), :]
-        if h >= 1:
-            y_direction(h - 1)
-    y_direction(len(groups) - 1)
+
+    lax.fori_loop(0, n_chunks, first_two, 0)
+    for load in loads[4:]:
+        load.wait()
+    x_direction(0)
+    x_direction(1)
+    make_b(2, 0, b_hi0, b_lo0)
+    one_more(2)
+    x_direction(2)
+    y_direction(0)
+    y_direction(1)
+    one_more(3)
+    x_direction(3)
+    y_direction(2)
+    y_direction(3)
 
     width = wzh.shape[1] // 2
     total = jnp.zeros((len_z, grid_n), jnp.float32)
@@ -262,6 +282,24 @@
         copy.wait_recv()
     send_r[...] = jnp.zeros_like(send_r)
     wide_m[...] = jnp.zeros_like(wide_m)
+    def start_sum(value, out, sums, sems, axis, ring, me):
+        out[...] = jnp.zeros_like(out) + value
+        copies = []
+        for k in range(1, len(ring)):
+            copy = remote(out, sums.at[me], sems.at[0, k], sems.at[1, k], {axis: ring[k]})
+            copy.start()
+            copies.append(copy)
+        sums[me] = jnp.zeros(out.shape, jnp.float32) + value
+        return copies
+
+    def end_sum(sums, copies):
+        for copy in copies:
+            copy.wait_recv()
+        result = sums[0]
+        for s in range(1, len(copies) + 1):
+            result = result + sums[s]
+        return result
+
     copies_m = []
     real_wide = jnp.concatenate([is_real] * z_devs, axis=1)
     for c, (first, last) in enumerate(chunks):
@@ -286,7 +324,7 @@
         for p in range(first, last, 2):
             for kx in (p, p + 1):
                 at = (kx - first) * rows_k
-                value = 0.5 * bc_ref[kx] * power[at:at + len_z, :grid_n]
+                value = bc_ref[kx] * power[at:at + len_z, :grid_n]
                 ek_ref[kx] = value
                 total = total + value
                 high, low = split_value(power_rev[at:at + rows_k, :])
@@ -294,36 +332,20 @@
                 if kx >= 1:
                     plane = len_x - kx - planes
                     factor = jnp.where(is_first, bc_row[plane, 0:1, :], bc_mirror[plane])
-                    value = 0.5 * factor * flipped[:len_z, :grid_n]
+                    value = factor * flipped[:len_z, :grid_n]
                     total = total + value
                     send_r[kx:kx + 1, :grid_n] = value[0:1, :]
                     wide_m[(kx - p) * rows_k:(kx - p) * rows_k + len_z, :grid_n] = value
             send_m[p * rows_k:(p + 2) * rows_k, :] = encode(wide_m[...], width - 1)
+        if last == planes:
+            copies_ez = start_sum(jnp.sum(total, keepdims=True), part, sums_z, sem_ez, 'zdom', ring_z, me_z)
+        rows = slice(max(first * rows_k, rows_k // 16 * 16), last * rows_k)
         copy = remote(send_m.at[rows, :], recv_m.at[rows, :], sem_sm.at[c], sem_rm.at[c], mirror)
         copy.start()
         copies_m.append(copy)
     copy_row = remote(send_r, recv_r, sem_row.at[0], sem_row.at[1], mirror_row)
     copy_row.start()
 
-    def start_sum(value, out, sums, sems, axis, ring, me):
-        out[...] = jnp.zeros_like(out) + value
-        copies = []
-        for k in range(1, len(ring)):
-            copy = remote(out, sums.at[me], sems.at[0, k], sems.at[1, k], {axis: ring[k]})
-            copy.start()
-            copies.append(copy)
-        sums[me] = jnp.zeros(out.shape, jnp.float32) + value
-        return copies
-
-    def end_sum(sums, copies):
-        for copy in copies:
-            copy.wait_recv()
-        result = sums[0]
-        for s in range(1, len(copies) + 1):
-            result = result + sums[s]
-        return result
-
-    copies_ez = start_sum(jnp.sum(total, keepdims=True), part, sums_z, sem_ez, 'zdom', ring_z, me_z)
     copies_ey = start_sum(end_sum(sums_z, copies_ez), part_z, sums_y, sem_ey, 'ydom', ring_y, me_y)
 
     copy_row.wait_recv()
@@ -336,7 +358,7 @@
                     at = (kx - p) * rows_k
                     ek_ref[len_x - kx] = jnp.where(is_first, recv_r[kx:kx + 1, :grid_n], both[at:at + len_z, :grid_n])
 
-    energy_ref[0] = end_sum(sums_y, copies_ey)[0, 0] / (grid_n * grid_n * grid_n)
+    energy_ref[0] = end_sum(sums_y, copies_ey)[0, 0] * 0.5 / (grid_n * grid_n * grid_n)
 
     for copy in copies_m + [copy_row] + copies_ez + copies_ey + copies_bc:
         copy.wait_send()
@@ -424,7 +446,7 @@
                 pltpu.VMEM((n_c, width, chunk), bf16), pltpu.VMEM((n_c, width, chunk), bf16),
                 *[pltpu.VMEM((rows_y * 16, chunk), bf16)] * 4,
                 pltpu.VMEM((n_c, 32, chunk), f32), pltpu.VMEM((n_c, 16 * n_g + 16, chunk), f32),
-                pltpu.VMEM((512, width), f32), pltpu.VMEM((y_devs * 4 * 40, LANES), f32),
+                pltpu.VMEM((2, 512, width), f32), pltpu.VMEM((y_devs * 4 * 40, LANES), f32),
                 pltpu.VMEM(influence.shape, f32), *[pltpu.VMEM(mat.shape, mat.dtype) for mat in mats],
                 pltpu.VMEM((n_g, y_devs * 128, LANES), i16),
                 pltpu.VMEM((n_g, y_devs, 128, LANES), i16),
@@ -448,6 +470,6 @@
                                                  vmem_limit_bytes=60 * 2**20),
         )(charge.reshape(1, slots), real_mask.reshape(1, slots), grid_idx.T, jnp.transpose(spline_w, (1, 2, 0)),
           influence, *mats)
-        return mode_energy, energy
+        return 0.5 * mode_energy, energy
 
     return jax.shard_map(local_energy, mesh=mesh, in_specs=(slot_spec, slot_spec, P(('sys', 'ydom', 'zdom'), None), P(('sys', 'ydom', 'zdom'), None, None), mode_spec), out_specs=(mode_spec, P('sys')), check_vma=False)

time: 90.1 us -> 87 us (0.966)
  Pallas kernels: 85 us -> 81.8 us
  other arithmetic: 0 us -> 2.63 us
  local copies, waits for them, and re-layouts: 2.63 us -> 0 us
    pallas_call x1, Pallas kernels: 85 us -> 81.8 us  [local_energy(): pl.pallas_call(functools.partial(energy_kernel, sizes), name='energy', ou...]
    mul x0 -> x1, other arithmetic: none -> 2.63 us  [local_energy(): return (0.5 * mode_energy, energy)]
    unnamed x1 -> x0, local copies, waits for them, and re-layouts: 2.63 us -> none
where the time goes in v4:
time: 87 us; the launch traced here: 86.8 us
  Pallas kernels  81.8 us (94%)
  other arithmetic  2.63 us (3%)
  between operations  2.37 us (3%)
    pallas_call x1, Pallas kernels, local_energy(): pl.pallas_call(functools.partial(energy_kernel, sizes), name='energy', ou...  81.8 us
    mul x1, other arithmetic, local_energy(): return (0.5 * mode_energy, energy)  2.63 us

profile of v4, /device:TPU:97, one launch (start us, length us, event | category | flops | bytes accessed | tf_op | source)
XLA Modules:
  0.0 86.8 jit_solution(16952995753156991637)
XLA Ops:
  0.6 81.8 %energy.1 = (f32[27,54,216]{2,1,0:T(8,128)}, f32[1]{0:T(128)}) custom-call(f32[1,8192]{1,0:T(1,128)} %bitcast.6, s32[1,8192]{1,0:T(1,128)} %bitcast.7, s32[3,8192]{1,0:T(4,128)} %bitcast.5, f32[3,4,8192]{2,1,0:T(4,128)} %bitcast.4, f32[27,54,216]{2,1,0:T(8,128)} %bc_hbm.1, bf16[256,256]{1,0:T(8,128)(2,1)} %constant.16.clone.fx_hi, ...), custom_call_target="tpu_custom_call" | custom-call | tf_op jit(solution)/shard_map/energy/pallas_call | solution.py:437
  82.5 2.6 %broadcast_multiply_fusion = f32[27,54,216]{2,1,0:T(8,128)} fusion(f32[27,54,216]{2,1,0:T(8,128)} %get-tuple-element.4), kind=kLoop, calls=%fused_computation | loop fusion | flops 314928 | bytes 2519424 | tf_op jit(solution)/shard_map/mul | solution.py:473
